TPU v7x, 128 devices: a 2x2x16 block of a 8x8x16 slice. The times are simulated.
128 devices in a mesh: groups: 4 (over x, y), blk: 32 (over z, core).
Axes of the slice: x: 2, y: 2, z: 16, core: 2. Of those that a mesh axis runs over, the one named last changes fastest.
The devices are a block of a 8x8x16 slice.
Arguments:
- pair_elements: float32 [49152, 1024], P(('groups', 'blk')), parts along dimension 0, may hold values from -0.8 to 0.8
- gmap: int32 [49152], P(('groups', 'blk')), parts along dimension 0, may hold values from 0 to 12287, as said below
- w_screened: float32 [49152, 12288], P('groups', 'blk'), parts along dimension 0, as said below
- coulomb: float32 [49152], P(('groups', 'blk')), parts along dimension 0, may hold values from 0.001 to 0.02
Outputs:
- screened: float32 [49152, 1024], P(('groups', 'blk')), parts along dimension 0
- pair_sigma: float32 [4096], P(('groups', 'blk')), parts along dimension 0
There are 4 independent parts, one for each index of `groups`. A program takes and returns all parts, laid end to end along the dimension named above; each array names one. Nothing has to cross between parts.
Inputs may be any that keep to these rules, and one draw needn't show every extreme that they name: `gmap`: each aligned block of 384 entries is a permutation of that block's own indices. `w_screened`: symmetric.
All inputs are finite; a program needn't handle non-finite values.
Results may differ from a plain program's by a relative error of at most 0.00013.
Values sent between devices are 32-bit elements; how exact they have to be, the bound alone decides.
A program may use at most 256 MiB of HBM per device.

v0:
```python
import jax
import jax.numpy as jnp
from jax import lax
from jax.sharding import PartitionSpec as P

NB = 64
OCC = 4


def cut_along(array, dim, devices):
    before, after = (array.shape[:dim], array.shape[dim + 1 :])
    return jnp.moveaxis(array.reshape(*before, devices, -1, *after), dim, 0)


def sum_at_owner(array, axis, dim):
    devices = lax.axis_size(axis)
    tiles = lax.all_to_all(cut_along(array, dim, devices), axis, 0, 0, tiled=True)
    return jnp.sum(tiles, axis=0)


def local(pair_elements, gmap, w_screened, coulomb):
    rows_here = pair_elements.shape[0]
    local_rows = gmap % rows_here
    elements = jnp.take(pair_elements, local_rows, axis=0)
    screened = lax.dot_general(
        w_screened,
        lax.all_gather(elements, "blk", axis=0, tiled=True),
        (((0,), (0,)), ((), ())),
        precision=lax.Precision.HIGHEST,
        preferred_element_type=jnp.float32,
    )
    band = jnp.arange(elements.shape[1], dtype=jnp.int32) % NB
    coef = jnp.where(band < OCC, -0.5, 0.5).astype(jnp.float32)
    partial_terms = coef * jnp.sum(screened * elements, axis=0) - 0.5 * jnp.sum(
        coulomb[:, None] * elements * elements, axis=0
    )
    pair_sigma = sum_at_owner(partial_terms, "blk", 0)
    return (screened, pair_sigma)


def solution(mesh):
    in_specs = (
        P(("groups", "blk"), None),
        P(("groups", "blk")),
        P("groups", "blk"),
        P(("groups", "blk")),
    )
    out_specs = (P(("groups", "blk"), None), P(("groups", "blk")))
    return jax.shard_map(local, mesh=mesh, in_specs=in_specs, out_specs=out_specs, check_vma=False)
```

profile of v0, /device:TPU:69, one launch (start us, length us, event | category | flops | bytes accessed | tf_op | source)
XLA Modules:
  0.0 387.6 jit_solution(10272636040177270883)
XLA Ops:
  7.2 0.0 copy-start
  7.2 0.1 all-gather.2.cloned.1.call-start
  7.3 0.8 compare_and_fusion
  8.1 0.5 copy-done
  8.6 1.8 gather_fusion
  10.4 1.3 broadcast_select_fusion
  11.8 0.0 copy-start.2
  11.8 0.0 copy-start.3
  11.8 0.1 all-gather.2.cloned.1.call-update
  11.8 279.4 %all-gather.2.cloned.1.call-done = f32[12288,1024]{1,0:T(8,128)} async-done(((f32[384,1024]{1,0:T(8,128)}), f32[12288,1024]{1,0:T(8,128)}) %all-gather.2.cloned.1.call-update) | async-done | bytes 50331664 | tf_op jit(solution)/shard_map/all_gather | solution.py:27
  291.2 0.0 copy-done.2
  291.2 0.0 copy-done.3
  291.2 0.0 copy-start.1
  291.2 67.6 %multiply_reduce_fusion = (f32[1024]{0:T(1024)S(1)}, f32[1024]{0:T(1024)S(1)}, f32[384,1024]{1,0:T(8,128)}) fusion(f32[384,1024]{1,0:T(8,128)S(1)} %copy-done.2, f32[384]{0:T(512)S(1)} %copy-done.3, f32[12288,1024]{1,0:T(8,128)} %all-gather.2.cloned.1.call-done, f32[12288,384]{1,0:T(8,128)} %param.6), kind=kOutput, calls=%fused_computation.3 | convolution fusion | flops 57984024576 | bytes 72361472 | tf_op jit(solution)/shard_map/dot_general | solution.py:25
  358.9 0.1 mul.46
  359.0 0.1 reduce_sum.30
  359.1 21.1 %all_to_all.6 = f32[32,1,32]{2,1,0:T(1,128)S(1)} all-to-all(f32[32,1,32]{2,1,0:T(1,128)S(1)} %fusion.2), channel_id=1, replica_groups=mesh['groups'=4,'blk'=32] {'blk'}, dimensions={0} | all-to-all | bytes 8192 | tf_op jit(solution)/shard_map/all_to_all | solution.py:17
  380.2 0.5 reduce_sum.32
  380.7 0.0 copy-done.1
  (3 shorter events, 0.0 us)
Async XLA Ops:
  7.2 1.4 copy-start
  7.2 284.0 %all-gather.2.cloned.1.call-start = ((), (), s32[]{:S(2)}) async-start(), calls=%async_computation.1 | async-start | bytes 51904512 | tf_op jit(solution)/shard_map/all_gather | solution.py:27
  11.8 279.5 %copy-start.2 = (f32[384,1024]{1,0:T(8,128)S(1)}, f32[384,1024]{1,0:T(8,128)}, u32[]{:S(2)}) copy-start(f32[384,1024]{1,0:T(8,128)} %broadcast_select_fusion) | copy-start | bytes 4718596
  11.8 279.5 %copy-start.3 = (f32[384]{0:T(512)S(1)}, f32[384]{0:T(512)}, u32[]{:S(2)}) copy-start(f32[384]{0:T(512)} %param.7) | copy-start | bytes 4612
  291.2 89.5 %copy-start.1 = (f32[384,1024]{1,0:T(8,128)S(1)}, f32[384,1024]{1,0:T(8,128)}, u32[]{:S(2)}) copy-start(f32[384,1024]{1,0:T(8,128)} %param.4) | copy-start | bytes 4718596
Sparse Core Ops, SparseCore 0:
  11.9 279.2 all-gather.1
where the time goes:
time: 388 us
  waiting for transfers between devices  279 us (72%)
  matrix products  67.6 us (17%)
  blocking collectives  21.1 us (5%)
  between operations  14.1 us (4%)
    all_gather x1, waiting for transfers between devices, local(): lax.all_gather(elements, 'blk', axis=0, tiled=True)  279 us
    dot_general x1, matrix products, local(): lax.dot_general(w_screened, lax.all_gather(elements, 'blk', axis=0, tiled...  67.6 us
    all_to_all x1, blocking collectives, sum_at_owner(): lax.all_to_all(cut_along(array, dim, devices), axis, 0, 0, tiled=True)  21.1 us
  transfers between devices with their start and end apart: 1, of which 1 were waited for; matrix products, arithmetic and copies ran while one was open for 0% of the time, Pallas kernels for 0%

commit v1 on v0

v1 whole, which is shorter than its diff:
```python
import functools

import jax
import jax.numpy as jnp
from jax import lax
from jax.experimental import pallas as pl
from jax.experimental.pallas import tpu as pltpu
from jax.sharding import PartitionSpec as P

NB = 64
OCC = 4
TILES = 4
MESH = pl.DeviceIdType.MESH


def split(x):
    hi = x.astype(jnp.bfloat16)
    return hi, (x - hi.astype(jnp.float32)).astype(jnp.bfloat16)


def dot(a, b):
    return jnp.dot(a, b, preferred_element_type=jnp.float32)


def kernel(
    devices,
    e_ref, w_ref, v_ref, out_ref, sig_ref,
    buf, wbuf, wt_hi, wt_lo, bare, terms, landed,
    ring_recv, pair_recv, right_send, left_send, pair_send, local_sem, w_sem, term_send, term_recv,
):
    rows, pairs = e_ref.shape
    width = pairs // TILES
    depth = devices // 2
    half = depth // 2
    group, me = lax.axis_index("groups"), lax.axis_index("blk")
    z, core = me // 2, me % 2

    def at(blk):
        return (group, blk)

    right = at(lax.rem(z + 1, depth) * 2 + core)
    left = at(lax.rem(z + depth - 1, depth) * 2 + core)
    partner = at(z * 2 + 1 - core)

    barrier = pltpu.get_barrier_semaphore()
    for other in (right, left, partner):
        pl.semaphore_signal(barrier, inc=1, device_id=other, device_id_type=MESH)

    def w_copy(i, block):
        source = pl.ds(pl.multiple_of(block * 2 * rows, 2 * rows), 2 * rows)
        return pltpu.make_async_copy(w_ref.at[source, :], wbuf.at[i % 2], w_sem.at[i % 2])

    def behind(s):
        return lax.rem(z + depth - s, depth)

    def ahead(s):
        return lax.rem(z + s, depth)

    def piece(source, which, k):
        start = pl.multiple_of((source * 2 + which) * rows, rows)
        return buf.at[k, pl.ds(start, rows), :]

    own_piece = [e_ref.at[:, pl.ds(k * width, width)] for k in range(TILES)]

    def ring_copy(src, source, k, send_sem, device):
        return pltpu.make_async_remote_copy(
            src_ref=src, dst_ref=piece(source, core, k), send_sem=send_sem.at[0],
            recv_sem=ring_recv.at[source, k], device_id=device, device_id_type=MESH)

    def pair_copy(src, source, which, k):
        return pltpu.make_async_remote_copy(
            src_ref=src, dst_ref=piece(source, which, k), send_sem=pair_send.at[0],
            recv_sem=pair_recv.at[source, k], device_id=partner, device_id_type=MESH)

    w_copy(0, z).start()
    w_copy(1, behind(1)).start()
    for k in range(TILES):
        pltpu.make_async_copy(own_piece[k], piece(z, core, k), local_sem.at[k]).start()
    pl.semaphore_wait(barrier, 3)
    for k in range(TILES):
        ring_copy(own_piece[k], z, k, right_send, right).start()
        ring_copy(own_piece[k], z, k, left_send, left).start()
        pair_copy(own_piece[k], z, core, k).start()

    def load_w(i, block):
        w_copy(i, block).wait()
        for part in range(2):
            cols = slice(part * rows, part * rows + rows)
            hi, lo = split(jnp.transpose(wbuf[i % 2, cols, :]))
            wt_hi[:, cols] = hi
            wt_lo[:, cols] = lo

    def product(k, block):
        start = pl.multiple_of(block * 2 * rows, 2 * rows)
        hi, lo = split(buf[k, pl.ds(start, 2 * rows), :])
        return dot(wt_hi[...], hi) + (dot(wt_hi[...], lo) + dot(wt_lo[...], hi))

    def tile(k):
        return pl.ds(pl.multiple_of(k * width, width), width)

    def add_block(block):
        def body(k, carry):
            out_ref[:, tile(k)] += product(k, block)
            return carry

        lax.fori_loop(0, TILES, body, 0)

    def pass_on(source, k, send_sem, device, onward):
        copy = ring_copy(piece(source, core, k), source, k, send_sem, device)
        copy.wait_recv()
        if onward is True:
            copy.start()
        elif onward is not False:
            pl.when(onward)(copy.start)
        pair_copy(piece(source, core, k), source, core, k).start()

    def take_pair(source, k):
        pair_copy(piece(source, 1 - core, k), source, 1 - core, k).wait_recv()

    load_w(0, z)
    w_copy(2, ahead(1)).start()
    for k in range(TILES):
        pltpu.make_async_copy(own_piece[k], piece(z, core, k), local_sem.at[k]).wait()
        take_pair(z, k)

    def first(k, carry):
        out_ref[:, tile(k)] = product(k, z)
        own = buf[k, pl.ds(pl.multiple_of(me * rows, rows), rows), :]
        bare[k] = jnp.dot(v_ref[...], own * own, precision=lax.Precision.HIGHEST, preferred_element_type=jnp.float32)
        return carry

    lax.fori_loop(0, TILES, first, 0)

    def step(s, carry):
        for k in range(TILES):
            on_right = True if k < TILES // 2 else s < half - 1
            on_left = True if k >= TILES // 2 else s < half - 1
            pass_on(behind(s), k, right_send, right, on_right)
            pass_on(ahead(s), k, left_send, left, on_left)
        load_w(1, behind(s))
        w_copy(1, behind(s + 1)).start()
        for k in range(TILES):
            take_pair(behind(s), k)
        add_block(behind(s))
        load_w(0, ahead(s))

        @pl.when(s < half - 1)
        def _():
            w_copy(0, ahead(s + 1)).start()

        for k in range(TILES):
            take_pair(ahead(s), k)
        add_block(ahead(s))
        return carry

    lax.fori_loop(1, half, step, 0)

    last = behind(half)
    load_w(1, last)
    lanes = terms.shape[-1]
    per_owner = pairs // devices
    owners_per_row = lanes // per_owner
    for j in range(TILES // 2):
        both = (j, TILES // 2 + j)
        pass_on(last, both[0], right_send, right, False)
        pass_on(last, both[1], left_send, left, False)
        for k in both:
            take_pair(last, k)
            cols = slice(k * width, (k + 1) * width)
            screened = out_ref[:, cols] + product(k, last)
            out_ref[:, cols] = screened
            own = buf[k, pl.ds(pl.multiple_of(me * rows, rows), rows), :]
            pair = lax.broadcasted_iota(jnp.int32, (1, width), 1) + k * width
            coef = jnp.where(pair % NB < OCC, -0.5, 0.5).astype(jnp.float32)
            term = coef * jnp.sum(screened * own, axis=0, keepdims=True) - 0.5 * bare[k]
            for r in range(width // lanes):
                terms[k * width // lanes + r] = term[:, r * lanes : (r + 1) * lanes]

    def term_copy(owner, slot):
        return pltpu.make_async_remote_copy(
            src_ref=terms.at[owner // owners_per_row], dst_ref=landed.at[slot], send_sem=term_send.at[0],
            recv_sem=term_recv.at[0], device_id=at(owner), device_id_type=MESH)

    def send_term(n, carry):
        owner = lax.rem(me + n, devices)
        term_copy(owner, lax.rem(me - owner - 1 + devices, devices)).start()
        return carry

    lax.fori_loop(1, devices, send_term, 0)

    whole = pltpu.make_async_copy(landed, landed, term_recv.at[0])
    whole.wait()
    total = terms[me // owners_per_row] + jnp.sum(landed[...], axis=0)
    place = me % owners_per_row
    mine = total[:, :per_owner]
    for r in range(1, owners_per_row):
        mine = jnp.where(place == r, total[:, r * per_owner : (r + 1) * per_owner], mine)
    sig_ref[...] = mine

    sent = pl.ds(0, (half - 1) * rows + rows // 2)
    for sem in (right_send, left_send):
        pltpu.make_async_copy(buf.at[:, sent, :], buf.at[:, sent, :], sem.at[0]).wait()
    sent = pl.ds(0, depth * rows)
    pltpu.make_async_copy(buf.at[:, sent, :], buf.at[:, sent, :], pair_send.at[0]).wait()
    pltpu.make_async_copy(landed, landed, term_send.at[0]).wait()


def local(devices, pair_elements, gmap, w_screened, coulomb):
    rows, pairs = pair_elements.shape
    elements = pair_elements.at[gmap % rows].get(mode="promise_in_bounds")
    width = pairs // TILES
    depth = devices // 2
    vmem = pl.BlockSpec(memory_space=pltpu.VMEM)
    hbm = pl.BlockSpec(memory_space=pl.ANY)
    screened, sigma = pl.pallas_call(
        functools.partial(kernel, devices),
        out_shape=(
            jax.ShapeDtypeStruct((rows, pairs), jnp.float32),
            jax.ShapeDtypeStruct((1, pairs // devices), jnp.float32),
        ),
        in_specs=[hbm, hbm, vmem],
        out_specs=(vmem, vmem),
        scratch_shapes=[
            pltpu.VMEM((TILES, devices * rows, width), jnp.float32),
            pltpu.VMEM((2, 2 * rows, rows), jnp.float32),
            pltpu.VMEM((rows, 2 * rows), jnp.bfloat16),
            pltpu.VMEM((rows, 2 * rows), jnp.bfloat16),
            pltpu.VMEM((TILES, 1, width), jnp.float32),
            pltpu.VMEM((pairs // 128, 1, 128), jnp.float32),
            pltpu.VMEM((devices - 1, 1, 128), jnp.float32),
            pltpu.SemaphoreType.DMA((depth, TILES)),
            pltpu.SemaphoreType.DMA((depth, TILES)),
            pltpu.SemaphoreType.DMA((1,)),
            pltpu.SemaphoreType.DMA((1,)),
            pltpu.SemaphoreType.DMA((1,)),
            pltpu.SemaphoreType.DMA((TILES,)),
            pltpu.SemaphoreType.DMA((2,)),
            pltpu.SemaphoreType.DMA((1,)),
            pltpu.SemaphoreType.DMA((1,)),
        ],
        compiler_params=pltpu.CompilerParams(
            collective_id=0, has_side_effects=True, vmem_limit_bytes=63 * 1024 * 1024
        ),
        name="ring_screen",
    )(elements, w_screened, coulomb[None, :])
    return screened, sigma.reshape(pairs // devices)


def solution(mesh):
    in_specs = (
        P(("groups", "blk"), None),
        P(("groups", "blk")),
        P("groups", "blk"),
        P(("groups", "blk")),
    )
    out_specs = (P(("groups", "blk"), None), P(("groups", "blk")))
    body = functools.partial(local, mesh.shape["blk"])
    return jax.shard_map(body, mesh=mesh, in_specs=in_specs, out_specs=out_specs, check_vma=False)
```

time: 388 us -> 292 us (0.75)
  Pallas kernels: 0 us -> 282 us
  waiting for transfers between devices: 279 us -> 0 us
  matrix products: 67.6 us -> 0 us
  blocking collectives: 21.1 us -> 0 us
  between operations: 14.1 us -> 0.65 us
  local copies, waits for them, and re-layouts: 2.55 us -> 9.32 us
    pallas_call x0 -> x1, Pallas kernels: none -> 282 us  [local(): pl.pallas_call(functools.partial(kernel, devices), out_shape=(jax.ShapeDt...]
    all_gather x1 -> x0, waiting for transfers between devices: 279 us -> none  [local(): lax.all_gather(elements, 'blk', axis=0, tiled=True)]
    dot_general x1 -> x0, matrix products: 67.6 us -> none  [local(): lax.dot_general(w_screened, lax.all_gather(elements, 'blk', axis=0, tiled...]
    all_to_all x1 -> x0, blocking collectives: 21.1 us -> none  [sum_at_owner(): lax.all_to_all(cut_along(array, dim, devices), axis, 0, 0, tiled=True)]
  transfers between devices with their start and end apart: 1 -> 0, of which waited for: 1 -> 0; matrix products, arithmetic and copies ran while one was open for 0% -> 0% of each run, Pallas kernels for 0% -> 0%
where the time goes in v1:
time: 292 us
  Pallas kernels  282 us (97%)
  local copies, waits for them, and re-layouts  9.32 us (3%)
    pallas_call x1, Pallas kernels, local(): pl.pallas_call(functools.partial(kernel, devices), out_shape=(jax.ShapeDt...  282 us

profile of v1, /device:TPU:69, one launch (start us, length us, event | category | flops | bytes accessed | tf_op | source)
XLA Modules:
  0.0 292.2 jit_solution(10098433206689711755)
XLA Ops:
  0.6 1.2 broadcast_in_dim.7.v_ref
  1.9 0.7 compare_select_fusion
  2.6 4.8 %gather_fusion = f32[384,1024]{1,0:T(8,128)} fusion(f32[384,1024]{1,0:T(8,128)} %param.4, s32[1024]{0:T(1024)S(1)} %pad_clamp_fusion), kind=kCustom, calls=%fused_computation | custom fusion | bytes 3147264 | tf_op jit(solution)/shard_map/gather | solution.py:210
  7.4 281.5 %ring_screen.1 = (f32[384,1024]{1,0:T(8,128)}, f32[1,32]{1,0:T(1,128)}) custom-call(f32[384,1024]{1,0:T(8,128)} %gather_fusion, f32[12288,384]{1,0:T(8,128)} %w_ref.1, f32[1,384]{1,0:T(1,128)} %broadcast_in_dim.7.v_ref), custom_call_target="tpu_custom_call" | custom-call | tf_op jit(solution)/shard_map/ring_screen/pallas_call | solution.py:215
  288.9 0.0 copy-start
  288.9 2.7 copy.8
  291.7 0.0 copy-done
  291.7 0.5 copy.9
  (1 shorter events, 0.0 us)
Async XLA Ops:
  288.9 2.7 copy-start

commit v2 on v1

v2 whole, which is shorter than its diff:
```python
import functools

import jax
import jax.numpy as jnp
from jax import lax
from jax.experimental import pallas as pl
from jax.experimental.pallas import tpu as pltpu
from jax.sharding import PartitionSpec as P

NB = 64
OCC = 4
TILES = 4
MESH = pl.DeviceIdType.MESH


def split(x):
    hi = x.astype(jnp.bfloat16)
    return hi, (x - hi.astype(jnp.float32)).astype(jnp.bfloat16)


def dot(a, b):
    return jnp.dot(a, b, preferred_element_type=jnp.float32)


def kernel(
    devices,
    e_ref, gmap_ref, w_ref, v_ref, out_ref, sig_ref,
    buf, wbuf, wt_hi, wt_lo, bare, twice, terms, landed,
    ring_recv, pair_recv, right_send, left_send, pair_send, local_sem, w_sem, term_send, term_recv,
):
    rows, pairs = e_ref.shape
    width = pairs // TILES
    depth = devices // 2
    half = depth // 2
    group, me = lax.axis_index("groups"), lax.axis_index("blk")
    z, core = me // 2, me % 2

    def at(blk):
        return (group, blk)

    right = at(lax.rem(z + 1, depth) * 2 + core)
    left = at(lax.rem(z + depth - 1, depth) * 2 + core)
    partner = at(z * 2 + 1 - core)

    barrier = pltpu.get_barrier_semaphore()
    for other in (right, left, partner):
        pl.semaphore_signal(barrier, inc=1, device_id=other, device_id_type=MESH)

    def w_copy(slot, block):
        source = pl.ds(pl.multiple_of(block * 2 * rows, 2 * rows), 2 * rows)
        return pltpu.make_async_copy(w_ref.at[source, :], wbuf.at[slot], w_sem.at[slot])

    def behind(s):
        return lax.rem(z + depth - s, depth)

    def ahead(s):
        return lax.rem(z + s, depth)

    def rows_of(blk):
        return pl.ds(pl.multiple_of(blk * rows, rows), rows)

    def piece(source, which, k):
        return buf.at[k, rows_of(source * 2 + which), :]

    def ring_copy(source, k, send_sem, device):
        return pltpu.make_async_remote_copy(
            src_ref=piece(source, core, k), dst_ref=piece(source, core, k), send_sem=send_sem.at[0],
            recv_sem=ring_recv.at[source, k], device_id=device, device_id_type=MESH)

    def pair_copy(source, which, k):
        return pltpu.make_async_remote_copy(
            src_ref=piece(source, which, k), dst_ref=piece(source, which, k), send_sem=pair_send.at[0],
            recv_sem=pair_recv.at[source, k], device_id=partner, device_id_type=MESH)

    def go_right(source, k):
        ring_copy(source, k, right_send, right).start()

    def go_left(source, k):
        ring_copy(source, k, left_send, left).start()

    def across(source, k):
        pair_copy(source, core, k).start()

    def from_left(source, k):
        ring_copy(source, k, right_send, right).wait_recv()

    def from_right(source, k):
        ring_copy(source, k, left_send, left).wait_recv()

    def take_pair(source, k):
        pair_copy(source, 1 - core, k).wait_recv()

    for k in (0, 3, 1, 2):
        cols = pl.ds(k * width, width)
        pltpu.make_async_copy(e_ref.at[:, cols], out_ref.at[:, cols], local_sem.at[k]).start()
    w_copy(0, z).start()
    w_copy(1, behind(1)).start()
    order = gmap_ref[...].reshape(1, rows) - me * rows
    chosen = (lax.broadcasted_iota(jnp.int32, (rows, rows), 0) == order).astype(jnp.float32)
    chosen = jnp.transpose(chosen).astype(jnp.bfloat16)

    def gather(k):
        cols = slice(k * width, (k + 1) * width)
        pltpu.make_async_copy(e_ref.at[:, cols], out_ref.at[:, cols], local_sem.at[k]).wait()
        raw = out_ref[:, cols]
        hi, rest = raw.astype(jnp.bfloat16), None
        rest = raw - hi.astype(jnp.float32)
        mid, low = split(rest)
        buf[k, rows_of(me), :] = (dot(chosen, hi) + dot(chosen, mid)) + dot(chosen, low)

    gather(0)
    gather(3)
    pl.semaphore_wait(barrier, 3)
    go_right(z, 0)
    go_left(z, 3)
    gather(1)
    gather(2)
    go_right(z, 1)
    go_left(z, 2)
    go_right(z, 2)
    go_left(z, 1)
    go_right(z, 3)
    go_left(z, 0)
    for k in range(TILES):
        across(z, k)

    def load_w(slot, block, to):
        w_copy(slot, block).wait()
        for part in range(2):
            cols = slice(part * rows, part * rows + rows)
            hi, lo = split(jnp.transpose(wbuf[slot, cols, :]))
            wt_hi[to, :, cols] = hi
            wt_lo[to, :, cols] = lo

    def product(k, block, w):
        start = pl.multiple_of(block * 2 * rows, 2 * rows)
        hi, lo = split(buf[k, pl.ds(start, 2 * rows), :])
        return dot(wt_hi[w], hi) + (dot(wt_hi[w], lo) + dot(wt_lo[w], hi))

    def own(k):
        return buf[k, rows_of(me), :]

    def tile(k):
        return pl.ds(pl.multiple_of(k * width, width), width)

    def add_block(block, w):
        def body(k, carry):
            out_ref[:, tile(k)] += product(k, block, w)
            return carry

        lax.fori_loop(0, TILES, body, 0)

    load_w(0, z, 0)
    w_copy(0, ahead(1)).start()
    for k in range(TILES):
        take_pair(z, k)

    def first(k, carry):
        out_ref[:, tile(k)] = product(k, z, 0)
        mine = own(k)
        bare[k] = jnp.dot(v_ref[...].reshape(1, rows), mine * mine, precision=lax.Precision.HIGHEST, preferred_element_type=jnp.float32)
        return carry

    lax.fori_loop(0, TILES, first, 0)

    def step(s, carry):
        for i in range(TILES):
            k = TILES - 1 - i
            from_left(behind(s), i)
            go_right(behind(s), i)
            across(behind(s), i)
            from_right(ahead(s), k)
            go_left(ahead(s), k)
            across(ahead(s), k)
        load_w(1, behind(s), 1)
        w_copy(1, behind(s + 1)).start()
        for k in range(TILES):
            take_pair(behind(s), k)
        add_block(behind(s), 1)
        load_w(0, ahead(s), 0)
        w_copy(0, ahead(s + 1)).start()
        for k in range(TILES):
            take_pair(ahead(s), k)
        add_block(ahead(s), 0)
        return carry

    lax.fori_loop(1, half - 2, step, 0)

    b6, a6, b7, a7, far = behind(half - 2), ahead(half - 2), behind(half - 1), ahead(half - 1), behind(half)
    for i in range(TILES):
        k = TILES - 1 - i
        from_left(b6, i)
        if i < 2:
            go_right(b6, i)
        across(b6, i)
        from_right(a6, k)
        if i < 2:
            go_left(a6, k)
        across(a6, k)
    load_w(1, b6, 1)
    w_copy(1, b7).start()
    for k in range(TILES):
        take_pair(b6, k)
    add_block(b6, 1)

    from_left(b7, 0)
    go_right(b7, 0)
    go_right(b6, 2)
    across(b7, 0)
    from_right(a7, 3)
    go_left(a7, 3)
    go_left(a6, 1)
    across(a7, 3)
    load_w(0, a6, 0)
    w_copy(0, a7).start()
    for k in range(TILES):
        take_pair(a6, k)
    add_block(a6, 0)

    from_left(b7, 1)
    go_right(b7, 1)
    go_right(b6, 3)
    across(b7, 1)
    from_right(a7, 2)
    go_left(a7, 2)
    go_left(a6, 0)
    across(a7, 2)
    load_w(1, b7, 1)
    w_copy(1, far).start()
    load_w(0, a7, 0)
    load_w(1, far, 2)

    def add(k, block, w):
        take_pair(block, k)
        cols = slice(k * width, (k + 1) * width)
        value = product(k, block, w)
        out_ref[:, cols] += value
        return value

    twice[0] = jnp.sum(add(0, b7, 1) * own(0), axis=0, keepdims=True)
    twice[1] = jnp.sum(add(3, a7, 0) * own(3), axis=0, keepdims=True)
    add(1, b7, 1)
    add(2, a7, 0)

    def arrive(source_left, k_left, source_right, k_right):
        from_left(source_left, k_left)
        across(source_left, k_left)
        from_right(source_right, k_right)
        across(source_right, k_right)

    arrive(far, 0, far, 3)
    add(0, far, 2)
    add(3, far, 2)
    arrive(b7, 2, a7, 1)
    add(2, b7, 1)
    add(1, a7, 0)
    arrive(far, 1, far, 2)
    add(1, far, 2)
    add(2, far, 2)

    lanes = terms.shape[-1]
    per_owner = pairs // devices
    owners_per_row = lanes // per_owner
    for k in range(TILES):
        total = jnp.sum(out_ref[:, k * width : (k + 1) * width] * own(k), axis=0, keepdims=True)
        if k == 0:
            total = total + twice[0]
        if k == 3:
            total = total + twice[1]
        pair = lax.broadcasted_iota(jnp.int32, (1, width), 1) + k * width
        coef = jnp.where(pair % NB < OCC, -0.5, 0.5).astype(jnp.float32)
        term = coef * total - 0.5 * bare[k]
        for r in range(width // lanes):
            terms[k * width // lanes + r] = term[:, r * lanes : (r + 1) * lanes]

    def term_copy(owner, slot):
        return pltpu.make_async_remote_copy(
            src_ref=terms.at[owner // owners_per_row], dst_ref=landed.at[slot], send_sem=term_send.at[0],
            recv_sem=term_recv.at[0], device_id=at(owner), device_id_type=MESH)

    def send_term(n, carry):
        owner = lax.rem(me + n, devices)
        term_copy(owner, lax.rem(me - owner - 1 + devices, devices)).start()
        return carry

    lax.fori_loop(1, devices, send_term, 0)

    arrive(b7, 3, a7, 0)
    add(3, b7, 1)
    add(0, a7, 0)

    pltpu.make_async_copy(landed, landed, term_recv.at[0]).wait()
    total = terms[me // owners_per_row] + jnp.sum(landed[...], axis=0)
    place = me % owners_per_row
    mine = total[:, :per_owner]
    for r in range(1, owners_per_row):
        mine = jnp.where(place == r, total[:, r * per_owner : (r + 1) * per_owner], mine)
    sig_ref[...] = mine

    sent = pl.ds(0, (half - 1) * rows + rows // 2)
    for sem in (right_send, left_send):
        pltpu.make_async_copy(buf.at[:, sent, :], buf.at[:, sent, :], sem.at[0]).wait()
    sent = pl.ds(0, depth * rows)
    pltpu.make_async_copy(buf.at[:, sent, :], buf.at[:, sent, :], pair_send.at[0]).wait()
    pltpu.make_async_copy(landed, landed, term_send.at[0]).wait()


def local(devices, pair_elements, gmap, w_screened, coulomb):
    rows, pairs = pair_elements.shape
    width = pairs // TILES
    depth = devices // 2
    vmem = pl.BlockSpec(memory_space=pltpu.VMEM)
    hbm = pl.BlockSpec(memory_space=pl.ANY)
    screened, sigma = pl.pallas_call(
        functools.partial(kernel, devices),
        out_shape=(
            jax.ShapeDtypeStruct((rows, pairs), jnp.float32),
            jax.ShapeDtypeStruct((1, pairs // devices), jnp.float32),
        ),
        in_specs=[hbm, vmem, hbm, vmem],
        out_specs=(vmem, vmem),
        scratch_shapes=[
            pltpu.VMEM((TILES, devices * rows, width), jnp.float32),
            pltpu.VMEM((2, 2 * rows, rows), jnp.float32),
            pltpu.VMEM((3, rows, 2 * rows), jnp.bfloat16),
            pltpu.VMEM((3, rows, 2 * rows), jnp.bfloat16),
            pltpu.VMEM((TILES, 1, width), jnp.float32),
            pltpu.VMEM((2, 1, width), jnp.float32),
            pltpu.VMEM((pairs // 128, 1, 128), jnp.float32),
            pltpu.VMEM((devices - 1, 1, 128), jnp.float32),
            pltpu.SemaphoreType.DMA((depth, TILES)),
            pltpu.SemaphoreType.DMA((depth, TILES)),
            pltpu.SemaphoreType.DMA((1,)),
            pltpu.SemaphoreType.DMA((1,)),
            pltpu.SemaphoreType.DMA((1,)),
            pltpu.SemaphoreType.DMA((TILES,)),
            pltpu.SemaphoreType.DMA((2,)),
            pltpu.SemaphoreType.DMA((1,)),
            pltpu.SemaphoreType.DMA((1,)),
        ],
        compiler_params=pltpu.CompilerParams(
            collective_id=0, has_side_effects=True, vmem_limit_bytes=63 * 1024 * 1024
        ),
        name="ring_screen",
    )(pair_elements, gmap, w_screened, coulomb)
    return screened, sigma.reshape(pairs // devices)


def solution(mesh):
    in_specs = (
        P(("groups", "blk"), None),
        P(("groups", "blk")),
        P("groups", "blk"),
        P(("groups", "blk")),
    )
    out_specs = (P(("groups", "blk"), None), P(("groups", "blk")))
    body = functools.partial(local, mesh.shape["blk"])
    return jax.shard_map(body, mesh=mesh, in_specs=in_specs, out_specs=out_specs, check_vma=False)
```

time: 292 us -> 281 us (0.962)
  local copies, waits for them, and re-layouts: 9.32 us -> 3.24 us
  Pallas kernels: 282 us -> 277 us
    gather x1 -> x0, local copies, waits for them, and re-layouts: 4.84 us -> none  [local(): elements = pair_elements.at[gmap % rows].get(mode='promise_in_bounds')]
    pallas_call x1, Pallas kernels: 282 us -> 277 us  [local(): pl.pallas_call(functools.partial(kernel, devices), out_shape=(jax.ShapeDt...]
where the time goes in v2:
time: 281 us
  Pallas kernels  277 us (99%)
  local copies, waits for them, and re-layouts  3.24 us (1%)
    pallas_call x1, Pallas kernels, local(): pl.pallas_call(functools.partial(kernel, devices), out_shape=(jax.ShapeDt...  277 us

profile of v2, /device:TPU:69, one launch (start us, length us, event | category | flops | bytes accessed | tf_op | source)
XLA Modules:
  0.0 281.0 jit_solution(16244830856670020320)
XLA Ops:
  0.6 277.1 %ring_screen.1 = (f32[384,1024]{1,0:T(8,128)}, f32[1,32]{1,0:T(1,128)}) custom-call(f32[384,1024]{1,0:T(8,128)} %e_ref.1, s32[384]{0:T(512)} %gmap_ref.1, f32[12288,384]{1,0:T(8,128)} %w_ref.1, f32[384]{0:T(512)} %v_ref.1), custom_call_target="tpu_custom_call" | custom-call | tf_op jit(solution)/shard_map/ring_screen/pallas_call | solution.py:314
  277.7 0.0 copy-start
  277.7 2.7 copy.8
  280.5 0.0 copy-done
  280.5 0.5 copy.9
Async XLA Ops:
  277.7 2.7 copy-start

commit v3 on v2

--- a/solution.py
+++ b/solution.py
@@ -96,8 +96,10 @@
     w_copy(0, z).start()
     w_copy(1, behind(1)).start()
     order = gmap_ref[...].reshape(1, rows) - me * rows
-    chosen = (lax.broadcasted_iota(jnp.int32, (rows, rows), 0) == order).astype(jnp.float32)
-    chosen = jnp.transpose(chosen).astype(jnp.bfloat16)
+    down = jnp.transpose(jnp.broadcast_to(order.astype(jnp.float32), (128, rows))).astype(jnp.int32)
+    lane = lax.broadcasted_iota(jnp.int32, (rows, 128), 1)
+    chosen = jnp.concatenate([(down == lane + at128).astype(jnp.float32) for at128 in range(0, rows, 128)], axis=1)
+    chosen = chosen.astype(jnp.bfloat16)
 
     def gather(k):
         cols = slice(k * width, (k + 1) * width)
@@ -187,14 +189,15 @@
     lax.fori_loop(1, half - 2, step, 0)
 
     b6, a6, b7, a7, far = behind(half - 2), ahead(half - 2), behind(half - 1), ahead(half - 1), behind(half)
+    before_wrap, after_first = z == depth - 1, z == 1
     for i in range(TILES):
         k = TILES - 1 - i
         from_left(b6, i)
-        if i < 2:
+        if i < 3:
             go_right(b6, i)
         across(b6, i)
         from_right(a6, k)
-        if i < 2:
+        if i < 3:
             go_left(a6, k)
         across(a6, k)
     load_w(1, b6, 1)
@@ -205,11 +208,9 @@
 
     from_left(b7, 0)
     go_right(b7, 0)
-    go_right(b6, 2)
     across(b7, 0)
     from_right(a7, 3)
     go_left(a7, 3)
-    go_left(a6, 1)
     across(a7, 3)
     load_w(0, a6, 0)
     w_copy(0, a7).start()
@@ -218,12 +219,20 @@
     add_block(a6, 0)
 
     from_left(b7, 1)
-    go_right(b7, 1)
+
+    @pl.when(jnp.logical_not(before_wrap))
+    def _():
+        go_right(b7, 1)
+
     go_right(b6, 3)
     across(b7, 1)
     from_right(a7, 2)
     go_left(a7, 2)
-    go_left(a6, 0)
+
+    @pl.when(jnp.logical_not(after_first))
+    def _():
+        go_left(a6, 0)
+
     across(a7, 2)
     load_w(1, b7, 1)
     w_copy(1, far).start()
@@ -248,12 +257,18 @@
         from_right(source_right, k_right)
         across(source_right, k_right)
 
+    arrive(b7, 2, a7, 1)
+
+    @pl.when(after_first)
+    def _():
+        go_left(a7, 1)
+        go_left(a6, 0)
+
+    add(2, b7, 1)
+    add(1, a7, 0)
     arrive(far, 0, far, 3)
     add(0, far, 2)
     add(3, far, 2)
-    arrive(b7, 2, a7, 1)
-    add(2, b7, 1)
-    add(1, a7, 0)
     arrive(far, 1, far, 2)
     add(1, far, 2)
     add(2, far, 2)
@@ -285,9 +300,18 @@
 
     lax.fori_loop(1, devices, send_term, 0)
 
+    def add_part(k, block, which, w):
+        hi, lo = split(buf[k, rows_of(block * 2 + which), :])
+        w_hi, w_lo = wt_hi[w, :, rows_of(which)], wt_lo[w, :, rows_of(which)]
+        out_ref[:, k * width : (k + 1) * width] += dot(w_hi, hi) + (dot(w_hi, lo) + dot(w_lo, hi))
+
     arrive(b7, 3, a7, 0)
-    add(3, b7, 1)
-    add(0, a7, 0)
+    add_part(3, b7, core, 1)
+    add_part(0, a7, core, 0)
+    take_pair(b7, 3)
+    add_part(3, b7, 1 - core, 1)
+    take_pair(a7, 0)
+    add_part(0, a7, 1 - core, 0)
 
     pltpu.make_async_copy(landed, landed, term_recv.at[0]).wait()
     total = terms[me // owners_per_row] + jnp.sum(landed[...], axis=0)
@@ -297,12 +321,32 @@
         mine = jnp.where(place == r, total[:, r * per_owner : (r + 1) * per_owner], mine)
     sig_ref[...] = mine
 
-    sent = pl.ds(0, (half - 1) * rows + rows // 2)
-    for sem in (right_send, left_send):
-        pltpu.make_async_copy(buf.at[:, sent, :], buf.at[:, sent, :], sem.at[0]).wait()
+    usual = (half - 1) * rows + rows // 2
+    piece_rows = rows // TILES
+    for sem, odd, count in ((right_send, before_wrap, usual - piece_rows), (left_send, after_first, usual + piece_rows)):
+
+        @pl.when(odd)
+        def _(sem=sem, count=count):
+            pltpu.make_async_copy(buf.at[:, pl.ds(0, count), :], buf.at[:, pl.ds(0, count), :], sem.at[0]).wait()
+
+        @pl.when(jnp.logical_not(odd))
+        def _(sem=sem):
+            pltpu.make_async_copy(buf.at[:, pl.ds(0, usual), :], buf.at[:, pl.ds(0, usual), :], sem.at[0]).wait()
+
     sent = pl.ds(0, depth * rows)
     pltpu.make_async_copy(buf.at[:, sent, :], buf.at[:, sent, :], pair_send.at[0]).wait()
     pltpu.make_async_copy(landed, landed, term_send.at[0]).wait()
+
+
+def put_out(screened_ref, sigma_ref, out_ref, sig_ref, sems):
+    copies = [
+        pltpu.make_async_copy(screened_ref, out_ref, sems.at[0]),
+        pltpu.make_async_copy(sigma_ref, sig_ref, sems.at[1]),
+    ]
+    for copy in copies:
+        copy.start()
+    for copy in copies:
+        copy.wait()
 
 
 def local(devices, pair_elements, gmap, w_screened, coulomb):
@@ -314,8 +358,8 @@
     screened, sigma = pl.pallas_call(
         functools.partial(kernel, devices),
         out_shape=(
-            jax.ShapeDtypeStruct((rows, pairs), jnp.float32),
-            jax.ShapeDtypeStruct((1, pairs // devices), jnp.float32),
+            pltpu.VMEM((rows, pairs), jnp.float32),
+            pltpu.VMEM((1, pairs // devices), jnp.float32),
         ),
         in_specs=[hbm, vmem, hbm, vmem],
         out_specs=(vmem, vmem),
@@ -339,10 +383,22 @@
             pltpu.SemaphoreType.DMA((1,)),
         ],
         compiler_params=pltpu.CompilerParams(
-            collective_id=0, has_side_effects=True, vmem_limit_bytes=63 * 1024 * 1024
+            collective_id=0, has_side_effects=True, vmem_limit_bytes=61 * 1024 * 1024
         ),
         name="ring_screen",
     )(pair_elements, gmap, w_screened, coulomb)
+    screened, sigma = pl.pallas_call(
+        put_out,
+        out_shape=(
+            jax.ShapeDtypeStruct((rows, pairs), jnp.float32),
+            jax.ShapeDtypeStruct((1, pairs // devices), jnp.float32),
+        ),
+        in_specs=[vmem, vmem],
+        out_specs=(hbm, hbm),
+        scratch_shapes=[pltpu.SemaphoreType.DMA((2,))],
+        compiler_params=pltpu.CompilerParams(vmem_limit_bytes=1024 * 1024),
+        name="put_out",
+    )(screened, sigma)
     return screened, sigma.reshape(pairs // devices)
 
 

time: 281 us -> 277 us (0.986)
  local copies, waits for them, and re-layouts: 3.24 us -> 0 us
    unnamed x4 -> x0, local copies, waits for them, and re-layouts: 3.24 us -> none
    pallas_call x1 -> x2, Pallas kernels: 277 us -> 276 us  [the longest x1 275 us: local(): pl.pallas_call(functools.partial(kernel, devices), out_shape=(pltpu.VMEM(...]
where the time goes in v3:
time: 277 us
  Pallas kernels  276 us (100%)
    pallas_call x1, Pallas kernels, local(): pl.pallas_call(functools.partial(kernel, devices), out_shape=(pltpu.VMEM(...  275 us

profile of v3, /device:TPU:69, one launch (start us, length us, event | category | flops | bytes accessed | tf_op | source)
XLA Modules:
  0.0 277.2 jit_solution(11720687324633308625)
XLA Ops:
  0.6 275.3 %ring_screen.1 = (f32[384,1024]{1,0:T(8,128)S(1)}, f32[1,32]{1,0:T(1,128)S(1)}) custom-call(f32[384,1024]{1,0:T(8,128)} %e_ref.1, s32[384]{0:T(512)} %gmap_ref.1, f32[12288,384]{1,0:T(8,128)} %w_ref.1, f32[384]{0:T(512)} %v_ref.1), custom_call_target="tpu_custom_call" | custom-call | tf_op jit(solution)/shard_map/ring_screen/pallas_call | solution.py:358
  275.9 1.2 put_out.1

commit v4 on v3

--- a/solution.py
+++ b/solution.py
@@ -26,7 +26,7 @@
     devices,
     e_ref, gmap_ref, w_ref, v_ref, out_ref, sig_ref,
     buf, wbuf, wt_hi, wt_lo, bare, twice, terms, landed,
-    ring_recv, pair_recv, right_send, left_send, pair_send, local_sem, w_sem, term_send, term_recv,
+    ring_recv, pair_recv, right_send, left_send, pair_send, local_sem, w_sem, term_send, term_recv, ready,
 ):
     rows, pairs = e_ref.shape
     width = pairs // TILES
@@ -42,9 +42,16 @@
     left = at(lax.rem(z + depth - 1, depth) * 2 + core)
     partner = at(z * 2 + 1 - core)
 
+    first_chip, after_first, opposite, before_wrap = z == 0, z == 1, z == half, z == depth - 1
+
     barrier = pltpu.get_barrier_semaphore()
-    for other in (right, left, partner):
+    for other in (left, partner):
         pl.semaphore_signal(barrier, inc=1, device_id=other, device_id_type=MESH)
+
+    @pl.when(jnp.logical_not(before_wrap))
+    def _():
+        pl.semaphore_signal(barrier, inc=1, device_id=right, device_id_type=MESH)
+
 
     def w_copy(slot, block):
         source = pl.ds(pl.multiple_of(block * 2 * rows, 2 * rows), 2 * rows)
@@ -110,19 +117,27 @@
         mid, low = split(rest)
         buf[k, rows_of(me), :] = (dot(chosen, hi) + dot(chosen, mid)) + dot(chosen, low)
 
+    def left_unless_first(*tiles):
+        @pl.when(jnp.logical_not(first_chip))
+        def _():
+            for k in tiles:
+                go_left(z, k)
+
     gather(0)
     gather(3)
-    pl.semaphore_wait(barrier, 3)
+    pl.semaphore_wait(barrier, jnp.where(first_chip, 2, 3))
+
+    @pl.when(before_wrap)
+    def _():
+        pl.semaphore_signal(ready, inc=1, device_id=right, device_id_type=MESH)
+
     go_right(z, 0)
-    go_left(z, 3)
+    left_unless_first(3)
     gather(1)
     gather(2)
-    go_right(z, 1)
-    go_left(z, 2)
-    go_right(z, 2)
-    go_left(z, 1)
-    go_right(z, 3)
-    go_left(z, 0)
+    for k in (1, 2, 3):
+        go_right(z, k)
+    left_unless_first(2, 1, 0)
     for k in range(TILES):
         across(z, k)
 
@@ -164,6 +179,12 @@
         return carry
 
     lax.fori_loop(0, TILES, first, 0)
+
+    @pl.when(first_chip)
+    def _():
+        pl.semaphore_wait(ready, 1)
+        for k in (3, 2, 1, 0):
+            go_left(z, k)
 
     def step(s, carry):
         for i in range(TILES):
@@ -186,59 +207,10 @@
         add_block(ahead(s), 0)
         return carry
 
-    lax.fori_loop(1, half - 2, step, 0)
-
-    b6, a6, b7, a7, far = behind(half - 2), ahead(half - 2), behind(half - 1), ahead(half - 1), behind(half)
-    before_wrap, after_first = z == depth - 1, z == 1
-    for i in range(TILES):
-        k = TILES - 1 - i
-        from_left(b6, i)
-        if i < 3:
-            go_right(b6, i)
-        across(b6, i)
-        from_right(a6, k)
-        if i < 3:
-            go_left(a6, k)
-        across(a6, k)
-    load_w(1, b6, 1)
-    w_copy(1, b7).start()
-    for k in range(TILES):
-        take_pair(b6, k)
-    add_block(b6, 1)
-
-    from_left(b7, 0)
-    go_right(b7, 0)
-    across(b7, 0)
-    from_right(a7, 3)
-    go_left(a7, 3)
-    across(a7, 3)
-    load_w(0, a6, 0)
-    w_copy(0, a7).start()
-    for k in range(TILES):
-        take_pair(a6, k)
-    add_block(a6, 0)
-
-    from_left(b7, 1)
-
-    @pl.when(jnp.logical_not(before_wrap))
-    def _():
-        go_right(b7, 1)
-
-    go_right(b6, 3)
-    across(b7, 1)
-    from_right(a7, 2)
-    go_left(a7, 2)
-
-    @pl.when(jnp.logical_not(after_first))
-    def _():
-        go_left(a6, 0)
-
-    across(a7, 2)
-    load_w(1, b7, 1)
-    w_copy(1, far).start()
-    load_w(0, a7, 0)
-    load_w(1, far, 2)
-
+    lax.fori_loop(1, half - 3, step, 0)
+
+    b5, b6, b7, far = (behind(half - n) for n in (3, 2, 1, 0))
+    a5, a6, a7 = (ahead(half - n) for n in (3, 2, 1))
     def add(k, block, w):
         take_pair(block, k)
         cols = slice(k * width, (k + 1) * width)
@@ -246,42 +218,99 @@
         out_ref[:, cols] += value
         return value
 
-    twice[0] = jnp.sum(add(0, b7, 1) * own(0), axis=0, keepdims=True)
-    twice[1] = jnp.sum(add(3, a7, 0) * own(3), axis=0, keepdims=True)
-    add(1, b7, 1)
-    add(2, a7, 0)
-
-    def arrive(source_left, k_left, source_right, k_right):
+    def add_part(k, block, which, w):
+        hi, lo = split(buf[k, rows_of(block * 2 + which), :])
+        w_hi, w_lo = wt_hi[w, :, rows_of(which)], wt_lo[w, :, rows_of(which)]
+        out_ref[:, k * width : (k + 1) * width] += dot(w_hi, hi) + (dot(w_hi, lo) + dot(w_lo, hi))
+
+    def share(value, k):
+        return jnp.sum(value * own(k), axis=0, keepdims=True)
+
+    def arrive(source_left, k_left, source_right, k_right, onward=False):
         from_left(source_left, k_left)
+        if onward:
+            go_right(source_left, k_left)
         across(source_left, k_left)
         from_right(source_right, k_right)
+        if onward:
+            go_left(source_right, k_right)
         across(source_right, k_right)
 
-    arrive(b7, 2, a7, 1)
-
-    @pl.when(after_first)
-    def _():
-        go_left(a7, 1)
-        go_left(a6, 0)
-
-    add(2, b7, 1)
-    add(1, a7, 0)
+    for i in range(TILES):
+        arrive(b5, i, a5, TILES - 1 - i, onward=i < 3)
+    load_w(1, b5, 1)
+    w_copy(1, b6).start()
+    for k in range(TILES):
+        take_pair(b5, k)
+    add_block(b5, 1)
+    arrive(b6, 0, a6, 3, onward=True)
+    load_w(0, a5, 0)
+    w_copy(0, a6).start()
+    for k in range(TILES):
+        take_pair(a5, k)
+    add_block(a5, 0)
+    arrive(b6, 1, a6, 2, onward=True)
+    go_right(b5, 3)
+    go_left(a5, 0)
+    load_w(1, b6, 1)
+    w_copy(1, b7).start()
+    load_w(0, a6, 0)
+    w_copy(0, a7).start()
+    add(0, b6, 1)
+    add(3, a6, 0)
+    add(1, b6, 1)
+    add(2, a6, 0)
+    arrive(b6, 2, a6, 1)
+    add(2, b6, 1)
+    add(1, a6, 0)
+    arrive(b7, 0, a7, 3, onward=True)
+    load_w(1, b7, 2)
+    w_copy(1, far).start()
+    load_w(0, a7, 3)
+    twice[0] = share(add(0, b7, 2), 0)
+    twice[3] = share(add(3, a7, 3), 3)
+    from_left(b7, 1)
+
+    @pl.when(jnp.logical_not(before_wrap))
+    def _():
+        go_right(b7, 1)
+
+    go_right(b6, 2)
+    across(b7, 1)
+    from_right(a7, 2)
+    go_left(a7, 2)
+    go_left(a6, 1)
+    across(a7, 2)
+    load_w(1, far, 4)
+    twice[1] = share(add(1, b7, 2), 1)
+    twice[2] = share(add(2, a7, 3), 2)
+    arrive(b6, 3, a6, 0, onward=True)
+    add(3, b6, 1)
+    add(0, a6, 0)
     arrive(far, 0, far, 3)
-    add(0, far, 2)
-    add(3, far, 2)
-    arrive(far, 1, far, 2)
-    add(1, far, 2)
-    add(2, far, 2)
+    add(0, far, 4)
+    add(3, far, 4)
+
+    @pl.when(jnp.logical_not(first_chip))
+    def _():
+        from_left(far, 1)
+        across(far, 1)
+
+    from_right(far, 2)
+    across(far, 2)
+
+    @pl.when(jnp.logical_not(first_chip))
+    def _():
+        far_share = share(add(1, far, 4), 1)
+        twice[1] += jnp.where(opposite, far_share, 0.0)
+
+    add(2, far, 4)
 
     lanes = terms.shape[-1]
     per_owner = pairs // devices
     owners_per_row = lanes // per_owner
     for k in range(TILES):
-        total = jnp.sum(out_ref[:, k * width : (k + 1) * width] * own(k), axis=0, keepdims=True)
-        if k == 0:
-            total = total + twice[0]
-        if k == 3:
-            total = total + twice[1]
+        total = share(out_ref[:, k * width : (k + 1) * width], k) + twice[k]
         pair = lax.broadcasted_iota(jnp.int32, (1, width), 1) + k * width
         coef = jnp.where(pair % NB < OCC, -0.5, 0.5).astype(jnp.float32)
         term = coef * total - 0.5 * bare[k]
@@ -300,18 +329,29 @@
 
     lax.fori_loop(1, devices, send_term, 0)
 
-    def add_part(k, block, which, w):
-        hi, lo = split(buf[k, rows_of(block * 2 + which), :])
-        w_hi, w_lo = wt_hi[w, :, rows_of(which)], wt_lo[w, :, rows_of(which)]
-        out_ref[:, k * width : (k + 1) * width] += dot(w_hi, hi) + (dot(w_hi, lo) + dot(w_lo, hi))
-
+    arrive(b7, 2, a7, 1)
+
+    @pl.when(after_first)
+    def _():
+        go_left(a7, 1)
+
+    add(2, b7, 2)
+    add(1, a7, 3)
     arrive(b7, 3, a7, 0)
-    add_part(3, b7, core, 1)
-    add_part(0, a7, core, 0)
+    add_part(3, b7, core, 2)
+    add_part(0, a7, core, 3)
     take_pair(b7, 3)
-    add_part(3, b7, 1 - core, 1)
+    add_part(3, b7, 1 - core, 2)
     take_pair(a7, 0)
-    add_part(0, a7, 1 - core, 0)
+    add_part(0, a7, 1 - core, 3)
+
+    @pl.when(first_chip)
+    def _():
+        from_right(far, 1)
+        across(far, 1)
+        add_part(1, far, core, 4)
+        take_pair(far, 1)
+        add_part(1, far, 1 - core, 4)
 
     pltpu.make_async_copy(landed, landed, term_recv.at[0]).wait()
     total = terms[me // owners_per_row] + jnp.sum(landed[...], axis=0)
@@ -366,10 +406,10 @@
         scratch_shapes=[
             pltpu.VMEM((TILES, devices * rows, width), jnp.float32),
             pltpu.VMEM((2, 2 * rows, rows), jnp.float32),
-            pltpu.VMEM((3, rows, 2 * rows), jnp.bfloat16),
-            pltpu.VMEM((3, rows, 2 * rows), jnp.bfloat16),
+            pltpu.VMEM((5, rows, 2 * rows), jnp.bfloat16),
+            pltpu.VMEM((5, rows, 2 * rows), jnp.bfloat16),
             pltpu.VMEM((TILES, 1, width), jnp.float32),
-            pltpu.VMEM((2, 1, width), jnp.float32),
+            pltpu.VMEM((TILES, 1, width), jnp.float32),
             pltpu.VMEM((pairs // 128, 1, 128), jnp.float32),
             pltpu.VMEM((devices - 1, 1, 128), jnp.float32),
             pltpu.SemaphoreType.DMA((depth, TILES)),
@@ -381,6 +421,7 @@
             pltpu.SemaphoreType.DMA((2,)),
             pltpu.SemaphoreType.DMA((1,)),
             pltpu.SemaphoreType.DMA((1,)),
+            pltpu.SemaphoreType.REGULAR,
         ],
         compiler_params=pltpu.CompilerParams(
             collective_id=0, has_side_effects=True, vmem_limit_bytes=61 * 1024 * 1024

time: 277 us -> 277 us (level)
  no operation moved by 1% of the time
where the time goes in v4:
time: 277 us
  Pallas kernels  276 us (100%)
    pallas_call x1, Pallas kernels, local(): pl.pallas_call(functools.partial(kernel, devices), out_shape=(pltpu.VMEM(...  275 us

profile of v4, /device:TPU:69, one launch (start us, length us, event | category | flops | bytes accessed | tf_op | source)
XLA Modules:
  0.0 277.3 jit_solution(16138255375106387081)
XLA Ops:
  0.6 275.3 %ring_screen.1 = (f32[384,1024]{1,0:T(8,128)S(1)}, f32[1,32]{1,0:T(1,128)S(1)}) custom-call(f32[384,1024]{1,0:T(8,128)} %e_ref.1, s32[384]{0:T(512)} %gmap_ref.1, f32[12288,384]{1,0:T(8,128)} %w_ref.1, f32[384]{0:T(512)} %v_ref.1), custom_call_target="tpu_custom_call" | custom-call | tf_op jit(solution)/shard_map/ring_screen/pallas_call | solution.py:398
  275.9 1.2 put_out.1

commit v5 on v4

--- a/solution.py
+++ b/solution.py
@@ -26,7 +26,7 @@
     devices,
     e_ref, gmap_ref, w_ref, v_ref, out_ref, sig_ref,
     buf, wbuf, wt_hi, wt_lo, bare, twice, terms, landed,
-    ring_recv, pair_recv, right_send, left_send, pair_send, local_sem, w_sem, term_send, term_recv, ready,
+    ring_recv, pair_recv, right_send, left_send, pair_send, local_sem, w_sem, term_send, term_recv, ready, cut_recv,
 ):
     rows, pairs = e_ref.shape
     width = pairs // TILES
@@ -42,7 +42,8 @@
     left = at(lax.rem(z + depth - 1, depth) * 2 + core)
     partner = at(z * 2 + 1 - core)
 
-    first_chip, after_first, opposite, before_wrap = z == 0, z == 1, z == half, z == depth - 1
+    first_chip, after_first, opposite_first = z == 0, z == 1, z == half
+    before_wrap, before_last, opposite_last = z == depth - 1, z == depth - 2, z == half - 1
 
     barrier = pltpu.get_barrier_semaphore()
     for other in (left, partner):
@@ -78,6 +79,22 @@
         return pltpu.make_async_remote_copy(
             src_ref=piece(source, which, k), dst_ref=piece(source, which, k), send_sem=pair_send.at[0],
             recv_sem=pair_recv.at[source, k], device_id=partner, device_id_type=MESH)
+
+    quarter = rows // 4
+
+    def cut_rows(source, which, k, over):
+        start = (source * 2 + which) * rows + (0 if over else quarter)
+        return buf.at[k, pl.ds(pl.multiple_of(start, 8), quarter if over else rows - quarter), :]
+
+    def cut_copy(source, k, over, send_sem, device):
+        return pltpu.make_async_remote_copy(
+            src_ref=cut_rows(source, core, k, over), dst_ref=cut_rows(source, core, k, over), send_sem=send_sem.at[0],
+            recv_sem=cut_recv.at[0 if over else 1], device_id=device, device_id_type=MESH)
+
+    def cut_pair(source, which, k, over):
+        return pltpu.make_async_remote_copy(
+            src_ref=cut_rows(source, which, k, over), dst_ref=cut_rows(source, which, k, over), send_sem=pair_send.at[0],
+            recv_sem=cut_recv.at[2 if over else 3], device_id=partner, device_id_type=MESH)
 
     def go_right(source, k):
         ring_copy(source, k, right_send, right).start()
@@ -275,16 +292,28 @@
     def _():
         go_right(b7, 1)
 
+    @pl.when(before_wrap)
+    def _():
+        cut_copy(b7, 1, True, right_send, right).start()
+
     go_right(b6, 2)
     across(b7, 1)
     from_right(a7, 2)
-    go_left(a7, 2)
+
+    @pl.when(jnp.logical_not(first_chip))
+    def _():
+        go_left(a7, 2)
+
+    @pl.when(first_chip)
+    def _():
+        cut_copy(a7, 2, True, left_send, left).start()
+
     go_left(a6, 1)
     across(a7, 2)
     load_w(1, far, 4)
     twice[1] = share(add(1, b7, 2), 1)
     twice[2] = share(add(2, a7, 3), 2)
-    arrive(b6, 3, a6, 0, onward=True)
+    arrive(b6, 3, a6, 0)
     add(3, b6, 1)
     add(0, a6, 0)
     arrive(far, 0, far, 3)
@@ -296,15 +325,26 @@
         from_left(far, 1)
         across(far, 1)
 
-    from_right(far, 2)
-    across(far, 2)
-
-    @pl.when(jnp.logical_not(first_chip))
-    def _():
-        far_share = share(add(1, far, 4), 1)
-        twice[1] += jnp.where(opposite, far_share, 0.0)
-
-    add(2, far, 4)
+    @pl.when(first_chip)
+    def _():
+        cut_copy(far, 1, True, right_send, right).wait_recv()
+        cut_pair(far, core, 1, True).start()
+
+    @pl.when(jnp.logical_not(before_wrap))
+    def _():
+        from_right(far, 2)
+        across(far, 2)
+
+    @pl.when(before_wrap)
+    def _():
+        cut_copy(far, 2, True, left_send, left).wait_recv()
+        cut_pair(far, core, 2, True).start()
+
+    for k, absent, opposite in ((1, first_chip, opposite_first), (2, before_wrap, opposite_last)):
+
+        @pl.when(jnp.logical_not(absent))
+        def _(k=k, opposite=opposite):
+            twice[k] += jnp.where(opposite, share(add(k, far, 4), k), 0.0)
 
     lanes = terms.shape[-1]
     per_owner = pairs // devices
@@ -328,12 +368,18 @@
         return carry
 
     lax.fori_loop(1, devices, send_term, 0)
+    go_right(b6, 3)
+    go_left(a6, 0)
 
     arrive(b7, 2, a7, 1)
 
+    @pl.when(before_last)
+    def _():
+        cut_copy(b7, 2, False, right_send, right).start()
+
     @pl.when(after_first)
     def _():
-        go_left(a7, 1)
+        cut_copy(a7, 1, False, left_send, left).start()
 
     add(2, b7, 2)
     add(1, a7, 3)
@@ -345,13 +391,16 @@
     take_pair(a7, 0)
     add_part(0, a7, 1 - core, 3)
 
-    @pl.when(first_chip)
-    def _():
-        from_right(far, 1)
-        across(far, 1)
-        add_part(1, far, core, 4)
-        take_pair(far, 1)
-        add_part(1, far, 1 - core, 4)
+    for k, absent in ((1, first_chip), (2, before_wrap)):
+
+        @pl.when(absent)
+        def _(k=k):
+            cut_copy(far, k, False, right_send, right).wait_recv()
+            cut_pair(far, core, k, False).start()
+            add_part(k, far, core, 4)
+            for over in (True, False):
+                cut_pair(far, 1 - core, k, over).wait_recv()
+            add_part(k, far, 1 - core, 4)
 
     pltpu.make_async_copy(landed, landed, term_recv.at[0]).wait()
     total = terms[me // owners_per_row] + jnp.sum(landed[...], axis=0)
@@ -362,16 +411,17 @@
     sig_ref[...] = mine
 
     usual = (half - 1) * rows + rows // 2
-    piece_rows = rows // TILES
-    for sem, odd, count in ((right_send, before_wrap, usual - piece_rows), (left_send, after_first, usual + piece_rows)):
-
-        @pl.when(odd)
-        def _(sem=sem, count=count):
-            pltpu.make_async_copy(buf.at[:, pl.ds(0, count), :], buf.at[:, pl.ds(0, count), :], sem.at[0]).wait()
-
-        @pl.when(jnp.logical_not(odd))
-        def _(sem=sem):
-            pltpu.make_async_copy(buf.at[:, pl.ds(0, usual), :], buf.at[:, pl.ds(0, usual), :], sem.at[0]).wait()
+    cut = (rows - quarter) // TILES
+    for sem, less, more in ((right_send, before_wrap, before_last), (left_send, first_chip, after_first)):
+        for case, count in (
+            (less, usual - cut),
+            (more, usual + cut),
+            (jnp.logical_not(jnp.logical_or(less, more)), usual),
+        ):
+
+            @pl.when(case)
+            def _(sem=sem, count=count):
+                pltpu.make_async_copy(buf.at[:, pl.ds(0, count), :], buf.at[:, pl.ds(0, count), :], sem.at[0]).wait()
 
     sent = pl.ds(0, depth * rows)
     pltpu.make_async_copy(buf.at[:, sent, :], buf.at[:, sent, :], pair_send.at[0]).wait()
@@ -422,6 +472,7 @@
             pltpu.SemaphoreType.DMA((1,)),
             pltpu.SemaphoreType.DMA((1,)),
             pltpu.SemaphoreType.REGULAR,
+            pltpu.SemaphoreType.DMA((4,)),
         ],
         compiler_params=pltpu.CompilerParams(
             collective_id=0, has_side_effects=True, vmem_limit_bytes=61 * 1024 * 1024

time: 277 us -> 277 us (level)
  no operation moved by 1% of the time
where the time goes in v5:
time: 277 us
  Pallas kernels  276 us (100%)
    pallas_call x1, Pallas kernels, local(): pl.pallas_call(functools.partial(kernel, devices), out_shape=(pltpu.VMEM(...  275 us

profile of v5, /device:TPU:69, one launch (start us, length us, event | category | flops | bytes accessed | tf_op | source)
XLA Modules:
  0.0 276.9 jit_solution(12412208179156631613)
XLA Ops:
  0.6 274.9 %ring_screen.1 = (f32[384,1024]{1,0:T(8,128)S(1)}, f32[1,32]{1,0:T(1,128)S(1)}) custom-call(f32[384,1024]{1,0:T(8,128)} %e_ref.1, s32[384]{0:T(512)} %gmap_ref.1, f32[12288,384]{1,0:T(8,128)} %w_ref.1, f32[384]{0:T(512)} %v_ref.1), custom_call_target="tpu_custom_call" | custom-call | tf_op jit(solution)/shard_map/ring_screen/pallas_call | solution.py:448
  275.6 1.2 put_out.1

commit v6 on v5

--- a/solution.py
+++ b/solution.py
@@ -114,7 +114,7 @@
     def take_pair(source, k):
         pair_copy(source, 1 - core, k).wait_recv()
 
-    for k in (0, 3, 1, 2):
+    for k in (3, 0, 2, 1):
         cols = pl.ds(k * width, width)
         pltpu.make_async_copy(e_ref.at[:, cols], out_ref.at[:, cols], local_sem.at[k]).start()
     w_copy(0, z).start()
@@ -140,16 +140,21 @@
             for k in tiles:
                 go_left(z, k)
 
+    @pl.when(before_wrap)
+    def _():
+        pl.semaphore_wait(barrier, 3)
+        pl.semaphore_signal(ready, inc=1, device_id=right, device_id_type=MESH)
+
+    gather(3)
+
+    @pl.when(jnp.logical_not(before_wrap))
+    def _():
+        pl.semaphore_wait(barrier, jnp.where(first_chip, 2, 3))
+
+    left_unless_first(3)
     gather(0)
-    gather(3)
-    pl.semaphore_wait(barrier, jnp.where(first_chip, 2, 3))
-
-    @pl.when(before_wrap)
-    def _():
-        pl.semaphore_signal(ready, inc=1, device_id=right, device_id_type=MESH)
 
     go_right(z, 0)
-    left_unless_first(3)
     gather(1)
     gather(2)
     for k in (1, 2, 3):

time: 277 us -> 277 us (level)
  no operation moved by 1% of the time
where the time goes in v6:
time: 277 us
  Pallas kernels  276 us (100%)
    pallas_call x1, Pallas kernels, local(): pl.pallas_call(functools.partial(kernel, devices), out_shape=(pltpu.VMEM(...  275 us

profile of v6, /device:TPU:69, one launch (start us, length us, event | category | flops | bytes accessed | tf_op | source)
XLA Modules:
  0.0 276.9 jit_solution(14446887217410026218)
XLA Ops:
  0.6 274.9 %ring_screen.1 = (f32[384,1024]{1,0:T(8,128)S(1)}, f32[1,32]{1,0:T(1,128)S(1)}) custom-call(f32[384,1024]{1,0:T(8,128)} %e_ref.1, s32[384]{0:T(512)} %gmap_ref.1, f32[12288,384]{1,0:T(8,128)} %w_ref.1, f32[384]{0:T(512)} %v_ref.1), custom_call_target="tpu_custom_call" | custom-call | tf_op jit(solution)/shard_map/ring_screen/pallas_call | solution.py:453
  275.5 1.2 put_out.1
